TPU v7x, 256 devices: a whole 4x4x8 slice. The times are simulated.
256 devices in a mesh: replica: 64 (over z, y, core), model: 4 (over x).
Axes of the slice: x: 4, y: 4, z: 8, core: 2. Of those that a mesh axis runs over, the one named last changes fastest.
Arguments:
- partial_up: float32 [64, 1024, 4096], P('replica', None, 'model'), may hold values from -8 to 8
- partial_down: float32 [64, 4096, 1024], P('replica', 'model'), may hold values from -8 to 8
- partial_norm: float32 [64, 1024], P('replica'), may hold values from -16 to 16
- partial_bias: float32 [64, 1024], P('replica'), may hold values from -16 to 16
- master_up: float32 [1024, 4096], P('replica', 'model'), may hold values from -0.1875 to 0.1875
- master_down: float32 [4096, 1024], P('model', 'replica'), may hold values from -0.09375 to 0.09375
- master_norm: float32 [1024], P('replica'), may hold values from 0.25 to 1.75
- master_bias: float32 [1024], P('replica'), may hold values from -3 to 3
- memory_up: float32 [1024, 4096], P('replica', 'model'), may hold values from 0.05 to 0.8
- memory_down: float32 [4096, 1024], P('model', 'replica'), may hold values from 0.05 to 0.8
- memory_norm: float32 [1024], P('replica'), may hold values from 0.05 to 0.8
- memory_bias: float32 [1024], P('replica'), may hold values from 0.05 to 0.8
Outputs:
- compute_up: bfloat16 [1024, 4096], P(None, 'model')
- compute_down: bfloat16 [4096, 1024], P('model')
- compute_norm: bfloat16 [1024], replicated
- compute_bias: bfloat16 [1024], replicated
- stepped_up: float32 [1024, 4096], P('replica', 'model')
- stepped_down: float32 [4096, 1024], P('model', 'replica')
- stepped_norm: float32 [1024], P('replica')
- stepped_bias: float32 [1024], P('replica')
- state_new_up: float32 [1024, 4096], P('replica', 'model')
- state_new_down: float32 [4096, 1024], P('model', 'replica')
- state_new_norm: float32 [1024], P('replica')
- state_new_bias: float32 [1024], P('replica')
All inputs are finite; a program needn't handle non-finite values.
Results may differ from a plain program's by a relative error of at most 0.001.
Values may be sent and summed in bfloat16 or wider, within the bound.
A program may use at most 128 MiB of HBM per device.

v0:
```python
import jax
import jax.numpy as jnp
from jax import lax
from jax.sharding import PartitionSpec as P

learn_rate = 0.05
hold_rate = 0.9


def in_blocks(shard, dim, size):
    before, after = (shard.shape[:dim], shard.shape[dim + 1 :])
    return jnp.moveaxis(shard.reshape(*before, size, -1, *after), dim, 0)


def sum_packed(arrays, axis, dims):
    size = lax.axis_size(axis)
    tiles = [in_blocks(a, dim, size) for a, dim in zip(arrays, dims)]
    lines = jnp.concatenate([b.reshape(size, -1) for b in tiles], axis=1)
    width = max(16, -(-lines.shape[1] // 1024) * 8)
    lines = jnp.pad(lines, ((0, 0), (0, width * 128 - lines.shape[1]))).reshape(-1, 128)
    line, at, done = (lax.psum_scatter(lines, axis, tiled=True).reshape(-1), 0, [])
    for b in tiles:
        part = b[0]
        done.append(line[at : at + part.size].reshape(part.shape))
        at += part.size
    return tuple(done)


def from_everyone(shard, axis):
    size = lax.axis_size(axis)
    return lax.all_to_all(
        jnp.broadcast_to(shard[None], (size, *shard.shape)), axis, 0, 0, tiled=True
    )


def over_copies(shard, axis):
    everything = from_everyone(shard, axis)
    return jnp.sum(everything, axis=0)


def packed_total(arrays, axis):
    ends = [0]
    for a in arrays:
        ends.append(ends[-1] + a.size)
    total = over_copies(jnp.concatenate([a.ravel() for a in arrays]), axis)
    return tuple((total[b:e].reshape(a.shape) for a, b, e in zip(arrays, ends, ends[1:])))


def gather_turned(arrays, axis, dims):
    turned = [jnp.moveaxis(a, dim, 0) for a, dim in zip(arrays, dims)]
    both = jnp.concatenate([t.reshape(len(t), -1) for t in turned], axis=1)
    out, at, done = (lax.all_gather(both, axis, axis=0, tiled=True), 0, [])
    for t, dim in zip(turned, dims):
        section = out[:, at : at + t[0].size].reshape(-1, *t.shape[1:])
        done.append(jnp.moveaxis(section, 0, dim))
        at += t[0].size
    return tuple(done)


def on_device(
    partial_up,
    partial_down,
    partial_norm,
    partial_bias,
    master_up,
    master_down,
    master_norm,
    master_bias,
    memory_up,
    memory_down,
    memory_norm,
    memory_bias,
):
    mean_up, mean_down = sum_packed((partial_up[0], partial_down[0]), "replica", (0, 1))
    whole_norm, whole_bias = packed_total((partial_norm[0], partial_bias[0]), "replica")
    place = lax.axis_index("replica")
    mean_norm = lax.dynamic_slice_in_dim(
        whole_norm, place * master_norm.shape[0], master_norm.shape[0]
    )
    mean_bias = lax.dynamic_slice_in_dim(
        whole_bias, place * master_bias.shape[0], master_bias.shape[0]
    )
    mean_rate = lax.axis_size("replica") ** (-0.5)
    mean_up = mean_up * mean_rate
    mean_down = mean_down * mean_rate
    mean_norm = mean_norm * mean_rate
    mean_bias = mean_bias * mean_rate
    state_new_up = hold_rate * memory_up + (1.0 - hold_rate) * mean_up * mean_up
    stepped_up = master_up - learn_rate * mean_up * lax.rsqrt(state_new_up + 1e-06)
    state_new_down = hold_rate * memory_down + (1.0 - hold_rate) * mean_down * mean_down
    stepped_down = master_down - learn_rate * mean_down * lax.rsqrt(state_new_down + 1e-06)
    state_new_norm = hold_rate * memory_norm + (1.0 - hold_rate) * mean_norm * mean_norm
    stepped_norm = master_norm - learn_rate * mean_norm * lax.rsqrt(state_new_norm + 1e-06)
    state_new_bias = hold_rate * memory_bias + (1.0 - hold_rate) * mean_bias * mean_bias
    stepped_bias = master_bias - learn_rate * mean_bias * lax.rsqrt(state_new_bias + 1e-06)
    compute_up, compute_down, compute_norm, compute_bias = gather_turned(
        (
            stepped_up.astype(jnp.bfloat16),
            stepped_down.astype(jnp.bfloat16),
            stepped_norm.astype(jnp.bfloat16),
            stepped_bias.astype(jnp.bfloat16),
        ),
        "replica",
        (0, 1, 0, 0),
    )
    return (
        compute_up,
        compute_down,
        compute_norm,
        compute_bias,
        stepped_up,
        stepped_down,
        stepped_norm,
        stepped_bias,
        state_new_up,
        state_new_down,
        state_new_norm,
        state_new_bias,
    )


def solution(mesh):
    in_specs = (
        P("replica", None, "model"),
        P("replica", "model", None),
        P("replica", None),
        P("replica", None),
        P("replica", "model"),
        P("model", "replica"),
        P("replica"),
        P("replica"),
        P("replica", "model"),
        P("model", "replica"),
        P("replica"),
        P("replica"),
    )
    out_specs = (
        P(None, "model"),
        P("model", None),
        P(),
        P(),
        P("replica", "model"),
        P("model", "replica"),
        P("replica"),
        P("replica"),
        P("replica", "model"),
        P("model", "replica"),
        P("replica"),
        P("replica"),
    )
    return jax.shard_map(
        on_device, mesh=mesh, in_specs=in_specs, out_specs=out_specs, check_vma=False
    )
```

profile of v0, /device:TPU:1, one launch (start us, length us, event | category | flops | bytes accessed | tf_op | source)
XLA Modules:
  0.0 303.0 jit_solution(8466722291256023141)
XLA Ops:
  7.2 0.0 reduce-scatter.2.cloned.1.call-start
  7.2 5.4 %copy.56 = f32[1,1024,1024]{1,2,0:T(8,128)} copy(f32[1,1024,1024]{2,1,0:T(8,128)} %param.13) | data formatting | bytes 8388608 | tf_op args[1]
  12.6 8.7 %copy.57 = f32[64,1024,16]{0,2,1:T(8,128)} copy(f32[64,1024,16]{1,2,0:T(8,128)} %bitcast.15) | data formatting | bytes 8388608 | tf_op jit(solution)/shard_map/transpose | solution.py:12
  21.3 6.8 %copy.58 = f32[64,16384]{1,0:T(8,128)} copy(f32[64,16384]{0,1:T(8,128)} %bitcast.14) | data formatting | bytes 8388608 | tf_op jit(solution)/shard_map/reshape | solution.py:18
  28.1 4.9 %reshape_reshape_squeeze.3 = f32[64,16384]{1,0:T(8,128)} reshape(f32[1,1024,1024]{2,1,0:T(8,128)} %param.12) | data formatting | bytes 8388608 | tf_op jit(solution)/shard_map/reshape;reshape;squeeze | solution.py:18
  33.0 7.3 %pad_maximum_fusion = f32[64,32768]{1,0:T(8,128)} fusion(f32[64,16384]{1,0:T(8,128)} %copy.58, f32[64,16384]{1,0:T(8,128)} %reshape_reshape_squeeze.3), kind=kLoop, calls=%fused_computation | loop fusion | flops 2097152 | bytes 16777216 | tf_op jit(solution)/shard_map/concatenate | solution.py:18
  40.3 9.3 %reshape.70 = f32[16384,128]{1,0:T(8,128)} reshape(f32[64,32768]{1,0:T(8,128)} %pad_maximum_fusion) | data formatting | bytes 16777216 | tf_op jit(solution)/shard_map/reshape | solution.py:20
  49.6 0.0 reduce-scatter.2.cloned.1.call-update
  49.7 0.6 copy-done.4
  50.3 0.0 copy-done.5
  50.3 1.1 broadcast_in_dim.2
  51.4 13.1 %all-to-all-start = ((f32[64,1,2048]{2,1,0:T(1,128)}), f32[64,1,2048]{2,1,0:T(1,128)S(1)}, u32[]{:S(2)}, u32[]{:S(2)}) async-start(f32[64,1,2048]{2,1,0:T(1,128)} %broadcast_in_dim.2), calls=%async_computation.1 | async-start | bytes 1048576 | tf_op jit(solution)/shard_map/all_to_all | solution.py:31
  64.5 0.0 all-gather.2.cloned.1.call-start
  64.6 17.6 %all-to-all-done = f32[64,1,2048]{2,1,0:T(1,128)S(1)} async-done(((f32[64,1,2048]{2,1,0:T(1,128)}), f32[64,1,2048]{2,1,0:T(1,128)S(1)}, u32[]{:S(2)}, u32[]{:S(2)}) %all-to-all-start) | async-done | bytes 524320 | tf_op jit(solution)/shard_map/all_to_all | solution.py:31
  82.2 0.3 reduce_sum.9
  82.6 0.6 convert_bitcast_fusion.1
  83.2 0.1 copy.62
  83.3 0.1 copy.63
  83.4 117.8 %reduce-scatter.2.cloned.1.call-done = f32[256,128]{1,0:T(8,128)} async-done(((f32[16384,128]{1,0:T(8,128)}), f32[256,128]{1,0:T(8,128)}) %reduce-scatter.2.cloned.1.call-update) | async-done | bytes 131088 | tf_op jit(solution)/shard_map/reduce_scatter | solution.py:21
  201.2 0.9 multiply_multiply_fusion
  202.1 0.2 mul.127
  202.3 0.2 copy.60
  202.5 0.2 mul.133
  202.7 0.2 copy.59
  202.8 0.7 fusion
  203.5 0.7 convert_bitcast_fusion
  204.2 0.7 concatenate.11
  204.9 0.0 all-gather.2.cloned.1.call-update
  204.9 82.8 %all-gather.2.cloned.1.call-done = bf16[1024,2050]{1,0:T(8,128)(2,1)} async-done(((bf16[16,2050]{1,0:T(8,128)(2,1)}), bf16[1024,2050]{1,0:T(8,128)(2,1)}) %all-gather.2.cloned.1.call-update) | async-done | bytes 4198416 | tf_op jit(solution)/shard_map/all_gather | solution.py:52
  287.7 4.0 %slice_bitcast_fusion = (bf16[1024,1024]{0,1:T(8,128)(2,1)S(1)}, bf16[1024,1024]{1,0:T(8,128)(2,1)}) fusion(bf16[1024,2050]{1,0:T(8,128)(2,1)} %all-gather.2.cloned.1.call-done), kind=kLoop, calls=%fused_computation.1 | loop fusion | bytes 8388608 | tf_op jit(solution)/shard_map/transpose | solution.py:55
  291.7 2.5 copy.64
  294.2 2.0 slice_reduce_fusion
  (22 shorter events, 0.1 us)
Async XLA Ops:
  7.2 194.0 %reduce-scatter.2.cloned.1.call-start = ((), (), s32[]{:S(2)}) async-start(), calls=%async_computation.2 | async-start | bytes 8519680 | tf_op jit(solution)/shard_map/reduce_scatter | solution.py:21
  49.6 0.7 copy-start.4
  49.6 0.7 copy-start.5
  49.6 32.9 %copy-start.6 = (f32[16]{0:T(128)S(1)}, f32[16]{0:T(128)}, u32[]{:S(2)}) copy-start(f32[16]{0:T(128)} %param.19) | copy-start | bytes 196
  49.6 32.9 %copy-start.7 = (f32[16]{0:T(128)S(1)}, f32[16]{0:T(128)}, u32[]{:S(2)}) copy-start(f32[16]{0:T(128)} %param.23) | copy-start | bytes 196
  49.6 32.9 %copy-start.8 = (f32[16]{0:T(128)S(1)}, f32[16]{0:T(128)}, u32[]{:S(2)}) copy-start(f32[16]{0:T(128)} %param.18) | copy-start | bytes 196
  49.6 32.9 %copy-start.9 = (f32[16]{0:T(128)S(1)}, f32[16]{0:T(128)}, u32[]{:S(2)}) copy-start(f32[16]{0:T(128)} %param.22) | copy-start | bytes 196
  49.7 153.2 %copy-start = (f32[16,1024]{1,0:T(8,128)S(1)}, f32[16,1024]{1,0:T(8,128)}, u32[]{:S(2)}) copy-start(f32[16,1024]{1,0:T(8,128)} %param.16) | copy-start | bytes 196612
  49.7 153.2 %copy-start.1 = (f32[16,1024]{1,0:T(8,128)S(1)}, f32[16,1024]{1,0:T(8,128)}, u32[]{:S(2)}) copy-start(f32[16,1024]{1,0:T(8,128)} %param.20) | copy-start | bytes 196612
  49.7 153.8 %copy-start.2 = (f32[1024,16]{0,1:T(8,128)S(1)}, f32[1024,16]{0,1:T(8,128)}, u32[]{:S(2)}) copy-start(f32[1024,16]{0,1:T(8,128)} %param.17) | copy-start | bytes 196612
  49.7 153.8 %copy-start.3 = (f32[1024,16]{0,1:T(8,128)S(1)}, f32[1024,16]{0,1:T(8,128)}, u32[]{:S(2)}) copy-start(f32[1024,16]{0,1:T(8,128)} %param.21) | copy-start | bytes 196612
  51.4 30.8 %all-to-all-start = ((f32[64,1,2048]{2,1,0:T(1,128)}), f32[64,1,2048]{2,1,0:T(1,128)S(1)}, u32[]{:S(2)}, u32[]{:S(2)}) async-start(f32[64,1,2048]{2,1,0:T(1,128)} %broadcast_in_dim.2), calls=%async_computation.1 | async-start | bytes 1048576 | tf_op jit(solution)/shard_map/all_to_all | solution.py:31
  64.5 223.2 %all-gather.2.cloned.1.call-start = ((), (), s32[]{:S(2)}) async-start(), calls=%async_computation.3 | async-start | bytes 4526080 | tf_op jit(solution)/shard_map/all_gather | solution.py:52
Sparse Core Ops, SparseCore 0:
  49.8 151.3 reduce-scatter.1
  205.1 82.5 all-gather.1
where the time goes:
time: 304 us; the launch traced here: 303 us
  waiting for transfers between devices  218 us (72%)
  local copies, waits for them, and re-layouts  46.9 us (15%)
  between operations  14.2 us (5%)
  starting transfers between devices  13.2 us (4%)
  other arithmetic  10.5 us (3%)
    reduce_scatter x1, waiting for transfers between devices, sum_packed(): lax.psum_scatter(lines, axis, tiled=True).reshape(-1)  118 us
    all_gather x1, waiting for transfers between devices, gather_turned(): out, at, done = (lax.all_gather(both, axis, axis=0, tiled=True), 0, [])  82.8 us
    all_to_all x1, waiting for transfers between devices, from_everyone(): lax.all_to_all(jnp.broadcast_to(shard[None], (size, *shard.shape)), axis,...  17.6 us
    all_to_all x1, starting transfers between devices, from_everyone(): lax.all_to_all(jnp.broadcast_to(shard[None], (size, *shard.shape)), axis,...  13.1 us
    reshape x1, local copies, waits for them, and re-layouts, sum_packed(): jnp.pad(lines, ((0, 0), (0, width * 128 - lines.shape[1]))).reshape(-1, 128)  9.25 us
    transpose x1, local copies, waits for them, and re-layouts, in_blocks(): return jnp.moveaxis(shard.reshape(*before, size, -1, *after), dim, 0)  8.7 us
    unnamed x22, local copies, waits for them, and re-layouts  8.56 us
    concatenate x1, other arithmetic, sum_packed(): lines = jnp.concatenate([b.reshape(size, -1) for b in tiles], axis=1)  7.3 us
  transfers between devices with their start and end apart: 3, of which 3 were waited for; matrix products, arithmetic and copies ran while one was open for 1% of the time, Pallas kernels for 0%

commit v1 on v0

v1 whole, which is shorter than its diff:
```python
import jax
import jax.numpy as jnp
from jax import lax
from jax.experimental import pallas as pl
from jax.experimental.pallas import tpu as pltpu
from jax.sharding import PartitionSpec as P

learn_rate = 0.05
hold_rate = 0.9
NZ, NY = 8, 4
MEAN_RATE = 64 ** (-0.5)
WAYS = ((0, 1), (1, -1))
F32, BF16 = jnp.float32, jnp.bfloat16


def adapt(total, master, memory):
    mean = total * MEAN_RATE
    state = hold_rate * memory + (1.0 - hold_rate) * mean * mean
    return master - learn_rate * mean * lax.rsqrt(state + 1e-06), state


def slot_of(step, piece, half):
    if step == 1:
        return 0
    return 2 * step - (2 if piece == half else 3)


def kernel(
    up, dn, norm, bias, mu, md, mn, mb, su, sd, sn, sb,
    cu, cd, cn, cb, tu, td, tn, tb, nu, nd, nn, nb,
    own_up, peer_up, own_dn, peer_dn, vecs, peer_vec,
    in_y, in_z, in_z2, turned, in_yd, pair,
    ou, od, part_dn, tile_dn,
    v_mu, v_md, v_su, v_sd, v_mn, v_mb, v_sn, v_sb,
    o_tu, o_td, o_nu, o_nd, o_tn, o_tb, o_nn, o_nb, o_cn, o_cb,
    load_up, load_dn, load_small, pass_up, pass_dn, pass_vec, got_up, got_dn, got_vec,
    y_out, y_in, z_out, z_in, z2_out, z2_in, yd_out, yd_in, pair_out, pair_in,
    tile_out, tile_in, gz_out, gz_in, uz_out, uz_in, uy_out, uy_in, uf_out, uf_in,
    dpass, dgot, upass, ugot, store_sem,
):
    me = lax.axis_index("replica")
    core = lax.rem(me, 2)
    row = lax.rem(me // 2, NY)
    lay = me // (2 * NY)
    other = 1 - core

    def place(z, y, c):
        return {"replica": (z * NY + y) * 2 + c}

    def zed(k):
        return lax.rem(lay + k + 2 * NZ, NZ)

    def why(k):
        return lax.rem(row + k + 2 * NY, NY)

    peer = place(lay, row, other)
    z_next = [place(zed(way), row, core) for _, way in WAYS]
    y_next = [place(lay, why(way), core) for _, way in WAYS]

    def remote(src, dst, out, arrive, where):
        return pltpu.make_async_remote_copy(
            src_ref=src, dst_ref=dst, send_sem=out, recv_sem=arrive,
            device_id=where, device_id_type=pl.DeviceIdType.MESH,
        )

    sent = []

    def go(copy):
        copy.start()
        sent.append(copy)
        return copy

    smalls = [
        (norm, vecs.at[0]), (bias, vecs.at[1]), (mu, v_mu), (md, v_md), (su, v_su), (sd, v_sd),
        (mn, v_mn), (mb, v_mb), (sn, v_sn), (sb, v_sb),
    ]
    small_copies = [
        pltpu.make_async_copy(a, b, load_small.at[i]) for i, (a, b) in enumerate(smalls)
    ]
    for c in small_copies:
        c.start()

    def up_piece(ky, p, c):
        return up.at[pl.ds(4 * p, 4), why(ky), c]

    def dn_piece(k, p, c):
        rows = pl.multiple_of(c * 512 + p * 256, 256)
        return dn.at[pl.ds(rows, 256), pl.ds(pl.multiple_of(zed(k) * 128, 128), 128)]

    dn_order = [(4, 0), (4, 1), (3, 1), (5, 0), (3, 0), (5, 1), (2, 0), (2, 1), (6, 0), (6, 1), (1, 0), (1, 1), (7, 0), (7, 1), (0, 0), (0, 1)]
    up_order = [(2, 0), (2, 1), (1, 1), (3, 0), (1, 0), (3, 1), (0, 0), (0, 1)]
    order = []
    for i in range(8):
        order += [("d",) + dn_order[2 * i], ("d",) + dn_order[2 * i + 1], ("u",) + up_order[i]]
    order = [("d", 4, 0), ("d", 4, 1), ("u", 2, 0), ("u", 2, 1), ("d", 3, 1), ("d", 5, 0), ("u", 1, 1), ("u", 3, 0)] + [
        o for o in order if o not in (("d", 4, 0), ("d", 4, 1), ("u", 2, 0), ("u", 2, 1), ("d", 3, 1), ("d", 5, 0), ("u", 1, 1), ("u", 3, 0))
    ]
    loads, passes = {}, {}
    for kind, k, p in order:
        if kind == "u":
            loads[kind, k, p] = pltpu.make_async_copy(
                up_piece(k, p, core), own_up.at[k, pl.ds(4 * p, 4)], load_up.at[k, p]
            )
            passes[kind, k, p] = remote(
                up_piece(k, p, other), peer_up.at[k, pl.ds(4 * p, 4)],
                pass_up.at[k, p], got_up.at[k, p], peer,
            )
        else:
            loads[kind, k, p] = pltpu.make_async_copy(
                dn_piece(k, p, core), own_dn.at[k, p, pl.ds(0, 256)], load_dn.at[k, p]
            )
            passes[kind, k, p] = remote(
                dn_piece(k, p, other), peer_dn.at[k, p], pass_dn.at[k, p], got_dn.at[k, p], peer
            )

    barrier = pltpu.get_barrier_semaphore()
    friends = [peer] + z_next
    for ky in (1, 2, 3):
        friends += [place(lay, why(ky), core), place(lay, why(ky), other)]
    for friend in friends:
        pl.semaphore_signal(barrier, inc=1, device_id=friend, device_id_type=pl.DeviceIdType.MESH)
    for key in order:
        loads[key].start()
    pl.semaphore_wait(barrier, len(friends))
    small_copies[0].wait()
    small_copies[1].wait()
    vec_pass = go(remote(vecs.at[other], peer_vec, pass_vec, got_vec, peer))
    for key in order:
        go(passes[key])

    vec_pass.wait_recv()
    peer_vec[...] = vecs[core] + peer_vec[...]

    def join(kind, k, p):
        loads[kind, k, p].wait()
        passes[kind, k, p].wait_recv()
        if kind == "u":
            own_up[k, 4 * p : 4 * p + 4] += peer_up[k, 4 * p : 4 * p + 4]
        else:
            own_dn[k, p, 0:256] += peer_dn[k, p]
            line = peer_vec[:, pl.ds(pl.multiple_of(zed(k) * 128, 128), 128)]
            own_dn[k, p, 256:264] = jnp.broadcast_to(line, (8, 128))

    def reducer(count, mine, arrive, out, inn, neighbour):
        reach = count // 2

        def chunk(way, step):
            return (way * (reach + 1 - step)) % count

        def send(way, step, piece):
            di, direction = way
            slot = slot_of(step, piece, di)
            go(remote(
                mine(chunk(direction, step), piece), arrive.at[di, slot],
                out.at[di, slot], inn.at[di, slot], neighbour[di],
            ))

        def take(way, step, piece):
            di, direction = way
            slot = slot_of(step, piece, di)
            remote(
                mine(chunk(direction, step), piece), arrive.at[di, slot],
                out.at[di, slot], inn.at[di, slot], neighbour[di],
            ).wait_recv()
            ref = mine(chunk(direction, step + 1), piece)
            ref[...] += arrive[di, slot]
            if step < reach:
                send(way, step + 1, piece)

        return send, take

    z_send, z_take = reducer(NZ, lambda k, p: own_dn.at[k, p], in_z, z_out, z_in, z_next)
    y_send, y_take = reducer(
        NY, lambda k, p: own_up.at[k, pl.ds(4 * p, 4)], in_y, y_out, y_in, y_next
    )
    z2_send, z2_take = reducer(
        NZ, lambda k, p: own_up.at[0, zed(k), pl.ds(8 * p, 8)], in_z2, z2_out, z2_in, z_next
    )
    yd_send, yd_take = reducer(
        NY,
        lambda k, p: turned.at[pl.ds(pl.multiple_of(16 * (2 * why(k) + p), 16), 16)],
        in_yd, yd_out, yd_in, y_next,
    )

    def both(act, step, near):
        for way in WAYS:
            act(way, step, way[0] if near else 1 - way[0])

    for p in (0, 1):
        join("d", 4, p)
    both(z_send, 1, True)
    for p in (0, 1):
        join("u", 2, p)
    both(y_send, 1, True)
    join("d", 3, 1)
    join("d", 5, 0)
    both(z_send, 2, False)
    join("u", 1, 1)
    join("u", 3, 0)
    both(y_send, 2, False)
    for key in order[8:]:
        if key[1] != 0:
            join(*key)
    both(z_take, 1, True)
    for key in order[8:]:
        if key[1] == 0:
            join(*key)
    both(y_take, 1, True)
    both(z_take, 2, False)
    both(z_take, 2, True)
    both(z_take, 3, False)
    both(y_take, 2, False)
    both(z_take, 3, True)
    both(y_take, 2, True)
    both(z2_send, 1, True)
    both(z2_send, 2, False)
    both(z_take, 4, False)
    both(z2_take, 1, True)
    both(z_take, 4, True)

    for p in (0, 1):
        turned[:, 256 * p : 256 * p + 256] = own_dn[0, p, 0:256].T
    turned[:, 512:640] = own_dn[0, 0, 136:264].T
    both(yd_send, 1, True)
    both(yd_send, 2, False)
    both(z2_take, 2, False)
    both(z2_take, 2, True)
    both(yd_take, 1, True)
    both(z2_take, 3, False)
    both(yd_take, 2, False)
    both(z2_take, 3, True)
    both(yd_take, 2, True)

    def mine_at(c):
        return pl.ds(pl.multiple_of(16 * (2 * row + c), 16), 16)

    pair_pass = go(remote(turned.at[mine_at(other)], pair.at[core], pair_out, pair_in, peer))
    pair[core] = turned[mine_at(core), :]
    for c in small_copies[2:]:
        c.wait()
    pair_pass.wait_recv()

    stores = []

    def keep(src, dst):
        copy = pltpu.make_async_copy(src, dst, store_sem.at[len(stores)])
        copy.start()
        stores.append(copy)

    lines = ((v_mn, v_sn, o_tn, o_nn, o_cn, cn, tn, nn), (v_mb, v_sb, o_tb, o_nb, o_cb, cb, tb, nb))
    for r in (0, 1):
        cols = slice(512 * r, 512 * r + 512)
        stepped, state = adapt(pair[r, :, 0:512], v_md[:, cols], v_sd[:, cols])
        o_td[:, cols] = stepped
        o_nd[:, cols] = state
        part_dn[r, :, 0:512] = stepped.astype(BF16)
        block = jnp.concatenate([pair[r, :, 512:640], jnp.zeros((112, 128), F32)], axis=0).T
        master, memory, o_t, o_n = lines[r][:4]
        stepped, state = adapt(block[127:128, 0:16], master[...], memory[...])
        o_t[...] = stepped
        o_n[...] = state
        wide = jnp.concatenate([stepped, jnp.zeros((1, 112), F32)], axis=1)
        part_dn[r, :, 512:640] = jnp.broadcast_to(wide, (128, 128)).T[0:16].astype(BF16)

    tile_copies = []
    for ky in range(NY):
        for x in (0, 1):
            if ky == 0 and x == 0:
                continue
            c = core if x == 0 else other
            tile_copies.append(go(remote(
                part_dn.at[c], tile_dn.at[2 * row + core], tile_out.at[ky, x], tile_in.at[ky, x],
                place(lay, why(ky), c),
            )))
    tile_dn[2 * row + core] = part_dn[core]
    both(z2_take, 4, False)
    both(z2_take, 4, True)
    stepped, state = adapt(own_up[0, lay], v_mu[...], v_su[...])
    o_tu[...] = stepped
    o_nu[...] = state
    ou[lay, row, core] = stepped.astype(BF16)

    def spread_up(way, step, piece):
        di, direction = way
        ref = ou.at[zed(-direction * (step - 1)), row, core, :, pl.ds(512 * piece, 512)]
        slot = 2 * step - (2 if piece == di else 1)
        return remote(ref, ref, uz_out.at[di, slot], uz_in.at[di, slot], z_next[di])

    def spread_dn(way, step, piece):
        di, direction = way
        rows = pl.ds(0, 256) if piece == 0 else pl.ds(256, 272)
        ref = od.at[zed(-direction * (step - 1)), core, rows]
        slot = 2 * step - (2 if piece == di else 1)
        return remote(ref, ref, gz_out.at[di, slot], gz_in.at[di, slot], z_next[di])

    def aside(di, kz):
        ref = ou.at[zed(kz), row, core]
        return remote(ref, ref, uy_out.at[di, kz % NZ], uy_in.at[di, kz % NZ], y_next[di])

    def aside_far(way, kz):
        di, direction = way
        ref = ou.at[zed(kz), why(-direction), core, :, pl.ds(512 * di, 512)]
        return remote(ref, ref, uf_out.at[di, kz % NZ], uf_in.at[di, kz % NZ], y_next[di])

    def across_dn(k):
        ref = od.at[zed(k), core]
        return remote(ref, ref, dpass.at[k % NZ], dgot.at[k % NZ], peer)

    def across_up(ky):
        ref = ou.at[:, why(ky), core]
        return remote(ref, ref, upass.at[ky], ugot.at[ky], peer)

    for way in WAYS:
        go(spread_up(way, 1, way[0]))
        go(spread_up(way, 1, 1 - way[0]))
    for di in (0, 1):
        go(aside(di, 0))

    for copy in tile_copies:
        copy.wait_recv()
    for j in range(5):
        flat = tile_dn[:, :, 128 * j : 128 * j + 128].astype(F32).reshape(128, 128).T.astype(BF16)
        if j < 4:
            od[lay, core, 128 * j : 128 * j + 128] = flat
        else:
            od[lay, core, 512:528] = flat[112:128]
    for way in WAYS:
        go(spread_dn(way, 1, way[0]))
        go(spread_dn(way, 1, 1 - way[0]))
    go(across_dn(0))

    def onward(spread, step):
        for near in (True, False):
            if step == 4 and not near:
                continue
            for way in WAYS:
                piece = way[0] if near else 1 - way[0]
                spread(way, step, piece).wait_recv()
                if step < 3 or (step == 3 and near):
                    go(spread(way, step + 1, piece))

    far = []
    for step in (1, 2, 3, 4):
        onward(spread_up, step)
        for kz in (step, -step) if step < 4 else (4,):
            for di in (0, 1):
                go(aside(di, kz))
        onward(spread_dn, step)
        for k in (step, -step) if step < 4 else (4,):
            go(across_dn(k))
        for kz in (step - 1, 1 - step) if step > 1 else (0,):
            for way in WAYS:
                aside(way[0], kz).wait_recv()
                far.append(go(aside_far(way, kz)))
    go(across_up(0))
    for kz in (4,):
        for way in WAYS:
            aside(way[0], kz).wait_recv()
            far.append(go(aside_far(way, kz)))
    go(across_up(1))
    go(across_up(3))
    for copy in far:
        copy.wait_recv()
    go(across_up(2))

    def keep_up(y, c):
        keep(ou.at[:, y, c], cu.at[:, y, c])

    def keep_dn(z, r):
        keep(
            od.at[z, r, pl.ds(0, 512)],
            cd.at[pl.ds(pl.multiple_of(512 * r, 512), 512), pl.ds(pl.multiple_of(128 * z, 128), 128)],
        )

    for a, b in ((o_tu, tu), (o_td, td), (o_nu, nu), (o_nd, nd), (o_tn, tn), (o_tb, tb), (o_nn, nn), (o_nb, nb)):
        keep(a, b)
    for ky in range(NY):
        keep_up(why(ky), core)
    for k in range(NZ):
        keep_dn(zed(k), core)
    for k in range(NZ):
        across_dn(k).wait_recv()
        keep_dn(zed(k), other)
    for z in range(NZ):
        o_cn[:, 128 * z : 128 * z + 128] = od[z, 0, 527:528]
        o_cb[:, 128 * z : 128 * z + 128] = od[z, 1, 527:528]
    keep(o_cn, cn)
    keep(o_cb, cb)
    for ky in (0, 1, 3, 2):
        across_up(ky).wait_recv()
        keep_up(why(ky), other)
    for copy in sent:
        copy.wait_send()
    for copy in stores:
        copy.wait()


def on_device(
    partial_up, partial_down, partial_norm, partial_bias,
    master_up, master_down, master_norm, master_bias,
    memory_up, memory_down, memory_norm, memory_bias,
):
    def shape(s, t=F32):
        return jax.ShapeDtypeStruct(s, t)

    def vm(*s, t=F32):
        return pltpu.VMEM(s, t)

    dma = pltpu.SemaphoreType.DMA
    anyw = pl.BlockSpec(memory_space=pl.ANY)
    out = pl.pallas_call(
        kernel,
        out_shape=(
            shape((NZ, NY, 2, 16, 1024), BF16), shape((1024, 1024), BF16),
            shape((1, 1024), BF16), shape((1, 1024), BF16),
            shape((16, 1024)), shape((16, 1024)), shape((1, 16)), shape((1, 16)),
            shape((16, 1024)), shape((16, 1024)), shape((1, 16)), shape((1, 16)),
        ),
        in_specs=[anyw] * 12,
        out_specs=(anyw,) * 12,
        scratch_shapes=[
            vm(NY, NZ, 16, 1024), vm(NY, NZ, 16, 1024),
            vm(NZ, 2, 264, 128), vm(NZ, 2, 256, 128), vm(2, 1, 1024), vm(1, 1024),
            vm(2, 3, 4, 16, 1024), vm(2, 7, 264, 128), vm(2, 7, 8, 1024),
            vm(128, 640), vm(2, 3, 16, 640), vm(2, 16, 640),
            vm(NZ, NY, 2, 16, 1024, t=BF16), vm(NZ, 2, 528, 128, t=BF16),
            vm(2, 16, 640, t=BF16), vm(8, 16, 640, t=BF16),
            vm(16, 1024), vm(16, 1024), vm(16, 1024), vm(16, 1024),
            vm(1, 16), vm(1, 16), vm(1, 16), vm(1, 16),
            vm(16, 1024), vm(16, 1024), vm(16, 1024), vm(16, 1024),
            vm(1, 16), vm(1, 16), vm(1, 16), vm(1, 16),
            vm(1, 1024, t=BF16), vm(1, 1024, t=BF16),
            dma((NY, 2)), dma((NZ, 2)), dma((10,)), dma((NY, 2)), dma((NZ, 2)), dma,
            dma((NY, 2)), dma((NZ, 2)), dma,
            dma((2, 3)), dma((2, 3)), dma((2, 7)), dma((2, 7)), dma((2, 7)), dma((2, 7)),
            dma((2, 3)), dma((2, 3)), dma, dma,
            dma((NY, 2)), dma((NY, 2)), dma((2, 7)), dma((2, 7)), dma((2, 7)), dma((2, 7)),
            dma((2, NZ)), dma((2, NZ)), dma((2, NZ)), dma((2, NZ)),
            dma((NZ,)), dma((NZ,)), dma((NY,)), dma((NY,)), dma((34,)),
        ],
        compiler_params=pltpu.CompilerParams(collective_id=0, has_side_effects=True),
        name="reduce_step_gather",
    )(
        partial_up.reshape(NZ, NY, 2, 16, 1024), partial_down[0], partial_norm, partial_bias,
        master_up, master_down.T, master_norm[None], master_bias[None],
        memory_up, memory_down.T, memory_norm[None], memory_bias[None],
    )
    cu, cd, cn, cb, tu, td, tn, tb, nu, nd, nn, nb = out
    return (
        cu.reshape(1024, 1024), cd, cn[0], cb[0],
        tu, td.T, tn[0], tb[0], nu, nd.T, nn[0], nb[0],
    )


def solution(mesh):
    in_specs = (
        P("replica", None, "model"), P("replica", "model", None), P("replica", None), P("replica", None),
        P("replica", "model"), P("model", "replica"), P("replica"), P("replica"),
        P("replica", "model"), P("model", "replica"), P("replica"), P("replica"),
    )
    out_specs = (
        P(None, "model"), P("model", None), P(), P(),
        P("replica", "model"), P("model", "replica"), P("replica"), P("replica"),
        P("replica", "model"), P("model", "replica"), P("replica"), P("replica"),
    )
    return jax.shard_map(
        on_device, mesh=mesh, in_specs=in_specs, out_specs=out_specs, check_vma=False
    )
```

time: 304 us -> 84.5 us (0.28)
  waiting for transfers between devices: 218 us -> 0 us
  Pallas kernels: 0 us -> 71.9 us
  local copies, waits for them, and re-layouts: 46.9 us -> 9.15 us
  between operations: 14.2 us -> 0.71 us
  starting transfers between devices: 13.2 us -> 0 us
  other arithmetic: 10.5 us -> 2.55 us
    reduce_scatter x1 -> x0, waiting for transfers between devices: 118 us -> none  [sum_packed(): lax.psum_scatter(lines, axis, tiled=True).reshape(-1)]
    all_gather x1 -> x0, waiting for transfers between devices: 82.8 us -> none  [gather_turned(): out, at, done = (lax.all_gather(both, axis, axis=0, tiled=True), 0, [])]
    pallas_call x0 -> x1, Pallas kernels: none -> 71.9 us  [on_device(): pl.pallas_call(kernel, out_shape=(shape((NZ, NY, 2, 16, 1024), BF16), sha...]
    all_to_all x1 -> x0, waiting for transfers between devices: 17.6 us -> none  [from_everyone(): lax.all_to_all(jnp.broadcast_to(shard[None], (size, *shard.shape)), axis,...]
    reshape x4 -> x0, local copies, waits for them, and re-layouts: 16.2 us -> none  [the longest x1 9.25 us: sum_packed(): jnp.pad(lines, ((0, 0), (0, width * 128 - lines.shape[1]))).reshape(-1, 128)]
    all_to_all x1 -> x0, starting transfers between devices: 13.1 us -> none  [from_everyone(): lax.all_to_all(jnp.broadcast_to(shard[None], (size, *shard.shape)), axis,...]
    transpose x2 -> x0, local copies, waits for them, and re-layouts: 12.7 us -> none  [the longest x1 8.7 us: in_blocks(): return jnp.moveaxis(shard.reshape(*before, size, -1, *after), dim, 0)]
    concatenate x2 -> x0, other arithmetic: 7.3 us -> none  [the longest x1 7.3 us: sum_packed(): lines = jnp.concatenate([b.reshape(size, -1) for b in tiles], axis=1)]
  transfers between devices with their start and end apart: 3 -> 0, of which waited for: 3 -> 0; matrix products, arithmetic and copies ran while one was open for 1% -> 0% of each run, Pallas kernels for 0% -> 0%
where the time goes in v1:
time: 84.5 us; the launch traced here: 84.3 us
  Pallas kernels  71.9 us (85%)
  local copies, waits for them, and re-layouts  9.15 us (11%)
  other arithmetic  2.55 us (3%)
    pallas_call x1, Pallas kernels, on_device(): pl.pallas_call(kernel, out_shape=(shape((NZ, NY, 2, 16, 1024), BF16), sha...  71.9 us
    unnamed x28, local copies, waits for them, and re-layouts  9.15 us
    pallas_call x2, other arithmetic, on_device(): pl.pallas_call(kernel, out_shape=(shape((NZ, NY, 2, 16, 1024), BF16), sha...  2.55 us

profile of v1, /device:TPU:1, one launch (start us, length us, event | category | flops | bytes accessed | tf_op | source)
XLA Modules:
  0.0 84.3 jit_solution(2909270736278845425)
XLA Ops:
  0.6 71.9 %reduce_step_gather.1 = (bf16[8,4,2,16,1024]{4,3,2,1,0:T(8,128)(2,1)}, bf16[1024,1024]{1,0:T(8,128)(2,1)}, bf16[1,1024]{1,0:T(2,128)(2,1)}, bf16[1,1024]{1,0:T(2...) custom-call(f32[8,4,2,16,1024]{4,3,2,1,0:T(8,128)} %bitcast.15, ...), custom_call_target="tpu_custom_call" | custom-call | tf_op jit(solution)/shard_map/reduce_step_gather/pallas_call | solution.py:411
  72.6 1.3 %reduce = bf16[1024]{0:T(1024)(128)(2,1)} reduce(bf16[1,1024]{1,0:T(2,128)(2,1)} %get-tuple-element.26, bf16[]{:T(256)} %constant.12), dimensions={0}, to_apply=%get-tuple-element.26.reduce_sub_computation | reduce | bytes 4098 | tf_op jit(solution)/shard_map/reduce_step_gather/pallas_call | solution.py:411
  73.9 1.3 %reduce.1 = bf16[1024]{0:T(1024)(128)(2,1)} reduce(bf16[1,1024]{1,0:T(2,128)(2,1)} %get-tuple-element.27, bf16[]{:T(256)} %constant.12), dimensions={0}, to_apply=%get-tuple-element.27.reduce_sub_computation | reduce | bytes 4098 | tf_op jit(solution)/shard_map/reduce_step_gather/pallas_call | solution.py:411
  75.1 0.0 copy-start
  75.1 3.2 %copy.34 = bf16[1024,1024]{1,0:T(8,128)(2,1)} copy(bf16[1024,1024]{1,0:T(8,128)(2,1)} %bitcast.17) | data formatting | bytes 4194304
  78.4 0.0 copy-done
  78.4 0.0 copy-start.4
  78.4 0.0 copy-start.3
  78.4 0.0 copy-start.8
  78.4 0.0 copy-start.7
  78.4 0.0 copy-start.2
  78.4 0.0 copy-start.1
  78.4 0.0 copy-start.6
  78.4 0.0 copy-start.5
  78.4 1.3 %copy.35 = bf16[1024,1024]{1,0:T(8,128)(2,1)} copy(bf16[1024,1024]{1,0:T(8,128)(2,1)S(1)} %copy-done) | data formatting | bytes 4194304
  79.7 0.0 copy-done.4
  79.7 0.6 copy.36
  80.4 0.0 copy-done.3
  80.4 0.6 copy.37
  81.0 0.0 copy-done.8
  81.0 0.5 copy.38
  81.5 0.0 copy-done.7
  81.5 0.5 copy.39
  82.0 0.0 copy-done.2
  82.0 0.6 copy.40
  82.7 0.0 copy-done.1
  82.7 0.6 copy.41
  83.3 0.0 copy-done.6
  83.3 0.5 copy.42
  83.8 0.0 copy-done.5
  83.8 0.5 copy.43
Async XLA Ops:
  75.1 3.2 %copy-start = (bf16[1024,1024]{1,0:T(8,128)(2,1)S(1)}, bf16[1024,1024]{1,0:T(8,128)(2,1)}, u32[]{:S(2)}) copy-start(bf16[1024,1024]{1,0:T(8,128)(2,1)} %get-tuple-element.49) | copy-start | bytes 6291460
  78.4 1.4 %copy-start.4 = (f32[16,1024]{1,0:T(8,128)S(1)}, f32[16,1024]{1,0:T(8,128)}, u32[]{:S(2)}) copy-start(f32[16,1024]{1,0:T(8,128)} %get-tuple-element.52) | copy-start | bytes 196612
  78.4 2.0 %copy-start.3 = (f32[16,1024]{1,0:T(8,128)S(1)}, f32[16,1024]{1,0:T(8,128)}, u32[]{:S(2)}) copy-start(f32[16,1024]{1,0:T(8,128)} %get-tuple-element.29) | copy-start | bytes 196612
  78.4 2.6 %copy-start.8 = (f32[1,16]{1,0:T(1,128)S(1)}, f32[1,16]{1,0:T(1,128)}, u32[]{:S(2)}) copy-start(f32[1,16]{1,0:T(1,128)} %get-tuple-element.30) | copy-start | bytes 196
  78.4 3.2 %copy-start.7 = (f32[1,16]{1,0:T(1,128)S(1)}, f32[1,16]{1,0:T(1,128)}, u32[]{:S(2)}) copy-start(f32[1,16]{1,0:T(1,128)} %get-tuple-element.31) | copy-start | bytes 196
  78.4 3.7 %copy-start.2 = (f32[16,1024]{1,0:T(8,128)S(1)}, f32[16,1024]{1,0:T(8,128)}, u32[]{:S(2)}) copy-start(f32[16,1024]{1,0:T(8,128)} %get-tuple-element.56) | copy-start | bytes 196612
  78.4 4.3 %copy-start.1 = (f32[16,1024]{1,0:T(8,128)S(1)}, f32[16,1024]{1,0:T(8,128)}, u32[]{:S(2)}) copy-start(f32[16,1024]{1,0:T(8,128)} %get-tuple-element.33) | copy-start | bytes 196612
  78.4 4.9 %copy-start.6 = (f32[1,16]{1,0:T(1,128)S(1)}, f32[1,16]{1,0:T(1,128)}, u32[]{:S(2)}) copy-start(f32[1,16]{1,0:T(1,128)} %get-tuple-element.34) | copy-start | bytes 196
  78.4 5.4 %copy-start.5 = (f32[1,16]{1,0:T(1,128)S(1)}, f32[1,16]{1,0:T(1,128)}, u32[]{:S(2)}) copy-start(f32[1,16]{1,0:T(1,128)} %get-tuple-element.35) | copy-start | bytes 196

commit v2 on v1

--- a/solution.py
+++ b/solution.py
@@ -27,16 +27,15 @@
 
 def kernel(
     up, dn, norm, bias, mu, md, mn, mb, su, sd, sn, sb,
-    cu, cd, cn, cb, tu, td, tn, tb, nu, nd, nn, nb,
+    ou, od, o_tu, o_td, o_nu, o_nd, o_tn, o_tb, o_nn, o_nb,
     own_up, peer_up, own_dn, peer_dn, vecs, peer_vec,
     in_y, in_z, in_z2, turned, in_yd, pair,
-    ou, od, part_dn, tile_dn,
+    part_dn, tile_dn,
     v_mu, v_md, v_su, v_sd, v_mn, v_mb, v_sn, v_sb,
-    o_tu, o_td, o_nu, o_nd, o_tn, o_tb, o_nn, o_nb, o_cn, o_cb,
     load_up, load_dn, load_small, pass_up, pass_dn, pass_vec, got_up, got_dn, got_vec,
     y_out, y_in, z_out, z_in, z2_out, z2_in, yd_out, yd_in, pair_out, pair_in,
     tile_out, tile_in, gz_out, gz_in, uz_out, uz_in, uy_out, uy_in, uf_out, uf_in,
-    dpass, dgot, upass, ugot, store_sem,
+    dpass, dgot, upass, ugot,
 ):
     me = lax.axis_index("replica")
     core = lax.rem(me, 2)
@@ -240,14 +239,7 @@
         c.wait()
     pair_pass.wait_recv()
 
-    stores = []
-
-    def keep(src, dst):
-        copy = pltpu.make_async_copy(src, dst, store_sem.at[len(stores)])
-        copy.start()
-        stores.append(copy)
-
-    lines = ((v_mn, v_sn, o_tn, o_nn, o_cn, cn, tn, nn), (v_mb, v_sb, o_tb, o_nb, o_cb, cb, tb, nb))
+    lines = ((v_mn, v_sn, o_tn, o_nn), (v_mb, v_sb, o_tb, o_nb))
     for r in (0, 1):
         cols = slice(512 * r, 512 * r + 512)
         stepped, state = adapt(pair[r, :, 0:512], v_md[:, cols], v_sd[:, cols])
@@ -255,7 +247,7 @@
         o_nd[:, cols] = state
         part_dn[r, :, 0:512] = stepped.astype(BF16)
         block = jnp.concatenate([pair[r, :, 512:640], jnp.zeros((112, 128), F32)], axis=0).T
-        master, memory, o_t, o_n = lines[r][:4]
+        master, memory, o_t, o_n = lines[r]
         stepped, state = adapt(block[127:128, 0:16], master[...], memory[...])
         o_t[...] = stepped
         o_n[...] = state
@@ -363,35 +355,38 @@
         copy.wait_recv()
     go(across_up(2))
 
-    def keep_up(y, c):
-        keep(ou.at[:, y, c], cu.at[:, y, c])
-
-    def keep_dn(z, r):
-        keep(
-            od.at[z, r, pl.ds(0, 512)],
-            cd.at[pl.ds(pl.multiple_of(512 * r, 512), 512), pl.ds(pl.multiple_of(128 * z, 128), 128)],
-        )
-
-    for a, b in ((o_tu, tu), (o_td, td), (o_nu, nu), (o_nd, nd), (o_tn, tn), (o_tb, tb), (o_nn, nn), (o_nb, nb)):
-        keep(a, b)
-    for ky in range(NY):
-        keep_up(why(ky), core)
-    for k in range(NZ):
-        keep_dn(zed(k), core)
     for k in range(NZ):
         across_dn(k).wait_recv()
-        keep_dn(zed(k), other)
-    for z in range(NZ):
-        o_cn[:, 128 * z : 128 * z + 128] = od[z, 0, 527:528]
-        o_cb[:, 128 * z : 128 * z + 128] = od[z, 1, 527:528]
-    keep(o_cn, cn)
-    keep(o_cb, cb)
-    for ky in (0, 1, 3, 2):
+    for ky in range(NY):
         across_up(ky).wait_recv()
-        keep_up(why(ky), other)
     for copy in sent:
         copy.wait_send()
-    for copy in stores:
+
+
+def writer(
+    ou, od, o_tu, o_td, o_nu, o_nd, o_tn, o_tb, o_nn, o_nb,
+    cu, cd, cn, cb, tu, td, tn, tb, nu, nd, nn, nb,
+    v_cn, v_cb, sem,
+):
+    pairs = [(ou, cu)]
+    for z in range(NZ):
+        for r in (0, 1):
+            pairs.append((
+                od.at[z, r, pl.ds(0, 512)], cd.at[pl.ds(512 * r, 512), pl.ds(128 * z, 128)]
+            ))
+    pairs += [
+        (o_tu, tu), (o_td, td), (o_nu, nu), (o_nd, nd), (o_tn, tn), (o_tb, tb), (o_nn, nn), (o_nb, nb),
+        (v_cn, cn), (v_cb, cb),
+    ]
+    copies = [pltpu.make_async_copy(a, b, sem.at[i]) for i, (a, b) in enumerate(pairs)]
+    for copy in copies[:-2]:
+        copy.start()
+    for r, line in enumerate((v_cn, v_cb)):
+        rows = [od[z, r, 520:528].astype(F32)[7:8] for z in range(NZ)]
+        line[...] = jnp.concatenate(rows, axis=0).astype(BF16)
+    for copy in copies[-2:]:
+        copy.start()
+    for copy in copies:
         copy.wait()
 
 
@@ -407,47 +402,63 @@
         return pltpu.VMEM(s, t)
 
     dma = pltpu.SemaphoreType.DMA
-    anyw = pl.BlockSpec(memory_space=pl.ANY)
-    out = pl.pallas_call(
+    hbm = pl.BlockSpec(memory_space=pltpu.HBM)
+    vmem = pl.BlockSpec(memory_space=pltpu.VMEM)
+    made = (
+        pltpu.VMEM((NZ, NY, 2, 16, 1024), BF16), pltpu.VMEM((NZ, 2, 528, 128), BF16),
+        vm(16, 1024), vm(16, 1024), vm(16, 1024), vm(16, 1024),
+        vm(1, 16), vm(1, 16), vm(1, 16), vm(1, 16),
+    )
+    made = pl.pallas_call(
         kernel,
-        out_shape=(
-            shape((NZ, NY, 2, 16, 1024), BF16), shape((1024, 1024), BF16),
-            shape((1, 1024), BF16), shape((1, 1024), BF16),
-            shape((16, 1024)), shape((16, 1024)), shape((1, 16)), shape((1, 16)),
-            shape((16, 1024)), shape((16, 1024)), shape((1, 16)), shape((1, 16)),
-        ),
-        in_specs=[anyw] * 12,
-        out_specs=(anyw,) * 12,
+        out_shape=made,
+        in_specs=[hbm] * 12,
+        out_specs=(vmem,) * 10,
         scratch_shapes=[
             vm(NY, NZ, 16, 1024), vm(NY, NZ, 16, 1024),
             vm(NZ, 2, 264, 128), vm(NZ, 2, 256, 128), vm(2, 1, 1024), vm(1, 1024),
             vm(2, 3, 4, 16, 1024), vm(2, 7, 264, 128), vm(2, 7, 8, 1024),
             vm(128, 640), vm(2, 3, 16, 640), vm(2, 16, 640),
-            vm(NZ, NY, 2, 16, 1024, t=BF16), vm(NZ, 2, 528, 128, t=BF16),
             vm(2, 16, 640, t=BF16), vm(8, 16, 640, t=BF16),
             vm(16, 1024), vm(16, 1024), vm(16, 1024), vm(16, 1024),
             vm(1, 16), vm(1, 16), vm(1, 16), vm(1, 16),
-            vm(16, 1024), vm(16, 1024), vm(16, 1024), vm(16, 1024),
-            vm(1, 16), vm(1, 16), vm(1, 16), vm(1, 16),
-            vm(1, 1024, t=BF16), vm(1, 1024, t=BF16),
             dma((NY, 2)), dma((NZ, 2)), dma((10,)), dma((NY, 2)), dma((NZ, 2)), dma,
             dma((NY, 2)), dma((NZ, 2)), dma,
             dma((2, 3)), dma((2, 3)), dma((2, 7)), dma((2, 7)), dma((2, 7)), dma((2, 7)),
             dma((2, 3)), dma((2, 3)), dma, dma,
             dma((NY, 2)), dma((NY, 2)), dma((2, 7)), dma((2, 7)), dma((2, 7)), dma((2, 7)),
             dma((2, NZ)), dma((2, NZ)), dma((2, NZ)), dma((2, NZ)),
-            dma((NZ,)), dma((NZ,)), dma((NY,)), dma((NY,)), dma((34,)),
+            dma((NZ,)), dma((NZ,)), dma((NY,)), dma((NY,)),
         ],
-        compiler_params=pltpu.CompilerParams(collective_id=0, has_side_effects=True),
+        compiler_params=pltpu.CompilerParams(
+            collective_id=0, has_side_effects=True, vmem_limit_bytes=32 * 1024 * 1024
+        ),
         name="reduce_step_gather",
-    )(
-        partial_up.reshape(NZ, NY, 2, 16, 1024), partial_down[0], partial_norm, partial_bias,
-        master_up, master_down.T, master_norm[None], master_bias[None],
-        memory_up, memory_down.T, memory_norm[None], memory_bias[None],
-    )
+    )(*(
+        pltpu.with_memory_space_constraint(a, pltpu.HBM)
+        for a in (
+            partial_up.reshape(NZ, NY, 2, 16, 1024), partial_down[0], partial_norm, partial_bias,
+            master_up, master_down.T, master_norm[None], master_bias[None],
+            memory_up, memory_down.T, memory_norm[None], memory_bias[None],
+        )
+    ))
+    out = pl.pallas_call(
+        writer,
+        out_shape=(
+            shape((NZ, NY, 2, 16, 1024), BF16), shape((1024, 1024), BF16),
+            shape((8, 128), BF16), shape((8, 128), BF16),
+            shape((16, 1024)), shape((16, 1024)), shape((1, 16)), shape((1, 16)),
+            shape((16, 1024)), shape((16, 1024)), shape((1, 16)), shape((1, 16)),
+        ),
+        in_specs=[vmem] * 10,
+        out_specs=(hbm,) * 12,
+        scratch_shapes=[vm(8, 128, t=BF16), vm(8, 128, t=BF16), dma((27,))],
+        compiler_params=pltpu.CompilerParams(vmem_limit_bytes=32 * 1024 * 1024),
+        name="write_out",
+    )(*made)
     cu, cd, cn, cb, tu, td, tn, tb, nu, nd, nn, nb = out
     return (
-        cu.reshape(1024, 1024), cd, cn[0], cb[0],
+        cu.reshape(1024, 1024), cd, cn.reshape(1024), cb.reshape(1024),
         tu, td.T, tn[0], tb[0], nu, nd.T, nn[0], nb[0],
     )
 

time: 84.5 us -> 74.2 us (0.88)
  local copies, waits for them, and re-layouts: 9.15 us -> 0 us
  other arithmetic: 2.55 us -> 0 us
  Pallas kernels: 71.9 us -> 73.4 us
    unnamed x28 -> x0, local copies, waits for them, and re-layouts: 9.15 us -> none
    pallas_call x2 -> x0, other arithmetic: 2.55 us -> none  [on_device(): pl.pallas_call(kernel, out_shape=(shape((NZ, NY, 2, 16, 1024), BF16), sha...]
    pallas_call x1 -> x2, Pallas kernels: 71.9 us -> 73.4 us  [the longest x1 71.1 us: on_device(): pl.pallas_call(kernel, out_shape=made, in_specs=[hbm] * 12, out_specs=(vm...]
where the time goes in v2:
time: 74.2 us; the launch traced here: 74.1 us
  Pallas kernels  73.4 us (99%)
    pallas_call x1, Pallas kernels, on_device(): pl.pallas_call(kernel, out_shape=made, in_specs=[hbm] * 12, out_specs=(vm...  71.1 us
    pallas_call x1, Pallas kernels, on_device(): pl.pallas_call(writer, out_shape=(shape((NZ, NY, 2, 16, 1024), BF16), sha...  2.32 us

profile of v2, /device:TPU:1, one launch (start us, length us, event | category | flops | bytes accessed | tf_op | source)
XLA Modules:
  0.0 74.1 jit_solution(11854539400417408107)
XLA Ops:
  0.6 71.1 %reduce_step_gather.1 = (bf16[8,4,2,16,1024]{4,3,2,1,0:T(8,128)(2,1)S(1)}, bf16[8,2,528,128]{3,2,1,0:T(8,128)(2,1)S(1)}, f32[16,1024]{1,0:T(8,128)S(1)}, f32[16,...) custom-call(f32[8,4,2,16,1024]{4,3,2,1,0:T(8,128)} %bitcast.17, ...), custom_call_target="tpu_custom_call" | custom-call | tf_op jit(solution)/shard_map/reduce_step_gather/pallas_call | solution.py:412
  71.8 2.3 %write_out.1 = (bf16[8,4,2,16,1024]{4,3,2,1,0:T(8,128)(2,1)}, bf16[1024,1024]{1,0:T(8,128)(2,1)}, bf16[8,128]{1,0:T(8,128)(2,1)}, bf16[8,128]{1,0:T(8,128)(2,1)}...) custom-call(bf16[8,4,2,16,1024]{4,3,2,1,0:T(8,128)(2,1)S(1)} %get-tu, ...), custom_call_target="tpu_custom_call" | custom-call | tf_op jit(solution)/shard_map/write_out/pallas_call | solution.py:445

commit v3 on v2

--- a/solution.py
+++ b/solution.py
@@ -19,6 +19,25 @@
     return master - learn_rate * mean * lax.rsqrt(state + 1e-06), state
 
 
+def wrap(x, most):
+    u = jnp.abs(x) * (224.0 / most)
+    u2 = u * u
+    u4 = u2 * u2
+    u8 = u4 * u4
+    y = jnp.where(u >= 1.0, u8 * u8, u8)
+    return jnp.where(x < 0, -y, y).astype(BF16)
+
+
+def unwrap(code, most):
+    y = code.astype(F32)
+    v = jnp.abs(y)
+    q = lax.rsqrt(lax.rsqrt(jnp.maximum(v, 1e-37)))
+    r8 = q * lax.rsqrt(q)
+    r16 = r8 * lax.rsqrt(r8)
+    r = jnp.where(v >= 1.0, r16, r8) * (most / 224.0)
+    return jnp.where(y > 0, r, jnp.where(y < 0, -r, 0.0))
+
+
 def slot_of(step, piece, half):
     if step == 1:
         return 0
@@ -29,11 +48,11 @@
     up, dn, norm, bias, mu, md, mn, mb, su, sd, sn, sb,
     ou, od, o_tu, o_td, o_nu, o_nd, o_tn, o_tb, o_nn, o_nb,
     own_up, peer_up, own_dn, peer_dn, vecs, peer_vec,
-    in_y, in_z, in_z2, turned, in_yd, pair,
+    in_y, in_z, in_z2, to_y, to_z, to_z2, turned, to_yd, in_yd, pair,
     part_dn, tile_dn,
     v_mu, v_md, v_su, v_sd, v_mn, v_mb, v_sn, v_sb,
     load_up, load_dn, load_small, pass_up, pass_dn, pass_vec, got_up, got_dn, got_vec,
-    y_out, y_in, z_out, z_in, z2_out, z2_in, yd_out, yd_in, pair_out, pair_in,
+    y_out, y_in, z_out, z_in, z2_out, z2_in, yd_out, yd_in,
     tile_out, tile_in, gz_out, gz_in, uz_out, uz_in, uy_out, uy_in, uf_out, uf_in,
     dpass, dgot, upass, ugot,
 ):
@@ -86,13 +105,10 @@
         rows = pl.multiple_of(c * 512 + p * 256, 256)
         return dn.at[pl.ds(rows, 256), pl.ds(pl.multiple_of(zed(k) * 128, 128), 128)]
 
-    dn_order = [(4, 0), (4, 1), (3, 1), (5, 0), (3, 0), (5, 1), (2, 0), (2, 1), (6, 0), (6, 1), (1, 0), (1, 1), (7, 0), (7, 1), (0, 0), (0, 1)]
-    up_order = [(2, 0), (2, 1), (1, 1), (3, 0), (1, 0), (3, 1), (0, 0), (0, 1)]
-    order = []
-    for i in range(8):
-        order += [("d",) + dn_order[2 * i], ("d",) + dn_order[2 * i + 1], ("u",) + up_order[i]]
-    order = [("d", 4, 0), ("d", 4, 1), ("u", 2, 0), ("u", 2, 1), ("d", 3, 1), ("d", 5, 0), ("u", 1, 1), ("u", 3, 0)] + [
-        o for o in order if o not in (("d", 4, 0), ("d", 4, 1), ("u", 2, 0), ("u", 2, 1), ("d", 3, 1), ("d", 5, 0), ("u", 1, 1), ("u", 3, 0))
+    order = [
+        ("d", 4, 0), ("d", 4, 1), ("u", 2, 0), ("u", 2, 1), ("d", 3, 1), ("d", 5, 0), ("u", 1, 1), ("u", 3, 0),
+        ("d", 3, 0), ("d", 5, 1), ("u", 1, 0), ("u", 3, 1), ("d", 2, 1), ("d", 6, 0), ("d", 2, 0), ("d", 6, 1),
+        ("d", 1, 1), ("d", 7, 0), ("d", 1, 0), ("d", 7, 1), ("u", 0, 0), ("u", 0, 1), ("d", 0, 0), ("d", 0, 1),
     ]
     loads, passes = {}, {}
     for kind, k, p in order:
@@ -128,7 +144,7 @@
         go(passes[key])
 
     vec_pass.wait_recv()
-    peer_vec[...] = vecs[core] + peer_vec[...]
+    peer_vec[...] = 0.5 * (vecs[core] + peer_vec[...])
 
     def join(kind, k, p):
         loads[kind, k, p].wait()
@@ -140,74 +156,74 @@
             line = peer_vec[:, pl.ds(pl.multiple_of(zed(k) * 128, 128), 128)]
             own_dn[k, p, 256:264] = jnp.broadcast_to(line, (8, 128))
 
-    def reducer(count, mine, arrive, out, inn, neighbour):
+    def reducer(count, mine, leave, arrive, out, inn, neighbour, most):
         reach = count // 2
 
         def chunk(way, step):
             return (way * (reach + 1 - step)) % count
 
+        def post(way, step, piece, value):
+            di = way[0]
+            slot = slot_of(step, piece, di)
+            leave[di, slot] = wrap(value, most * (step if piece == di else step - 1))
+            go(remote(
+                leave.at[di, slot], arrive.at[di, slot], out.at[di, slot], inn.at[di, slot], neighbour[di]
+            ))
+
         def send(way, step, piece):
-            di, direction = way
-            slot = slot_of(step, piece, di)
-            go(remote(
-                mine(chunk(direction, step), piece), arrive.at[di, slot],
-                out.at[di, slot], inn.at[di, slot], neighbour[di],
-            ))
+            post(way, step, piece, mine(chunk(way[1], step), piece)[...])
 
         def take(way, step, piece):
             di, direction = way
             slot = slot_of(step, piece, di)
             remote(
-                mine(chunk(direction, step), piece), arrive.at[di, slot],
-                out.at[di, slot], inn.at[di, slot], neighbour[di],
+                leave.at[di, slot], arrive.at[di, slot], out.at[di, slot], inn.at[di, slot], neighbour[di]
             ).wait_recv()
             ref = mine(chunk(direction, step + 1), piece)
-            ref[...] += arrive[di, slot]
+            total = ref[...] + unwrap(arrive[di, slot], most * (step if piece == di else step - 1))
             if step < reach:
-                send(way, step + 1, piece)
+                post(way, step + 1, piece, total)
+            else:
+                ref[...] = total
 
         return send, take
 
-    z_send, z_take = reducer(NZ, lambda k, p: own_dn.at[k, p], in_z, z_out, z_in, z_next)
+    z_send, z_take = reducer(
+        NZ, lambda k, p: own_dn.at[k, p], to_z, in_z, z_out, z_in, z_next, 16.0
+    )
     y_send, y_take = reducer(
-        NY, lambda k, p: own_up.at[k, pl.ds(4 * p, 4)], in_y, y_out, y_in, y_next
+        NY, lambda k, p: own_up.at[k, pl.ds(4 * p, 4)], to_y, in_y, y_out, y_in, y_next, 16.0
     )
     z2_send, z2_take = reducer(
-        NZ, lambda k, p: own_up.at[0, zed(k), pl.ds(8 * p, 8)], in_z2, z2_out, z2_in, z_next
-    )
-    yd_send, yd_take = reducer(
-        NY,
-        lambda k, p: turned.at[pl.ds(pl.multiple_of(16 * (2 * why(k) + p), 16), 16)],
-        in_yd, yd_out, yd_in, y_next,
+        NZ, lambda k, p: own_up.at[0, zed(k), :, pl.ds(512 * p, 512)],
+        to_z2, in_z2, z2_out, z2_in, z_next, 64.0,
     )
 
     def both(act, step, near):
         for way in WAYS:
             act(way, step, way[0] if near else 1 - way[0])
 
-    for p in (0, 1):
-        join("d", 4, p)
+    def joins(*keys):
+        for key in keys:
+            join(*key)
+
+    joins(*order[:2])
     both(z_send, 1, True)
-    for p in (0, 1):
-        join("u", 2, p)
+    joins(*order[2:4])
     both(y_send, 1, True)
-    join("d", 3, 1)
-    join("d", 5, 0)
+    joins(*order[4:6])
     both(z_send, 2, False)
-    join("u", 1, 1)
-    join("u", 3, 0)
+    joins(*order[6:8])
     both(y_send, 2, False)
-    for key in order[8:]:
-        if key[1] != 0:
-            join(*key)
+    joins(*order[8:10])
     both(z_take, 1, True)
-    for key in order[8:]:
-        if key[1] == 0:
-            join(*key)
+    joins(*order[10:14])
+    both(z_take, 2, False)
     both(y_take, 1, True)
-    both(z_take, 2, False)
+    joins(*order[14:18])
     both(z_take, 2, True)
     both(z_take, 3, False)
+    joins(*order[18:])
     both(y_take, 2, False)
     both(z_take, 3, True)
     both(y_take, 2, True)
@@ -220,25 +236,29 @@
     for p in (0, 1):
         turned[:, 256 * p : 256 * p + 256] = own_dn[0, p, 0:256].T
     turned[:, 512:640] = own_dn[0, 0, 136:264].T
-    both(yd_send, 1, True)
-    both(yd_send, 2, False)
+    to_yd[...] = wrap(turned[...], 128.0).reshape(8, 16, 640)
+    others = [(ky, x) for ky in (2, 1, 3, 0) for x in (0, 1) if (ky, x) != (0, 0)]
+    shares = {}
+    for ky, x in others:
+        c = core if x == 0 else other
+        shares[ky, x] = go(remote(
+            to_yd.at[2 * why(ky) + c], in_yd.at[core, ky], yd_out.at[ky, x], yd_in.at[ky, x],
+            place(lay, why(ky), c),
+        ))
     both(z2_take, 2, False)
     both(z2_take, 2, True)
-    both(yd_take, 1, True)
     both(z2_take, 3, False)
-    both(yd_take, 2, False)
-    both(z2_take, 3, True)
-    both(yd_take, 2, True)
-
-    def mine_at(c):
-        return pl.ds(pl.multiple_of(16 * (2 * row + c), 16), 16)
-
-    pair_pass = go(remote(turned.at[mine_at(other)], pair.at[core], pair_out, pair_in, peer))
-    pair[core] = turned[mine_at(core), :]
+    for key in others:
+        shares[key].wait_recv()
+    pair[core] = turned[pl.ds(pl.multiple_of(16 * (2 * row + core), 16), 16), :] + (
+        unwrap(in_yd[core, 1], 128.0) + unwrap(in_yd[core, 2], 128.0) + unwrap(in_yd[core, 3], 128.0)
+    )
+    pair[other] = (
+        unwrap(in_yd[other, 0], 128.0) + unwrap(in_yd[other, 1], 128.0)
+        + unwrap(in_yd[other, 2], 128.0) + unwrap(in_yd[other, 3], 128.0)
+    )
     for c in small_copies[2:]:
         c.wait()
-    pair_pass.wait_recv()
-
     lines = ((v_mn, v_sn, o_tn, o_nn), (v_mb, v_sb, o_tb, o_nb))
     for r in (0, 1):
         cols = slice(512 * r, 512 * r + 512)
@@ -248,7 +268,7 @@
         part_dn[r, :, 0:512] = stepped.astype(BF16)
         block = jnp.concatenate([pair[r, :, 512:640], jnp.zeros((112, 128), F32)], axis=0).T
         master, memory, o_t, o_n = lines[r]
-        stepped, state = adapt(block[127:128, 0:16], master[...], memory[...])
+        stepped, state = adapt(2.0 * block[127:128, 0:16], master[...], memory[...])
         o_t[...] = stepped
         o_n[...] = state
         wide = jnp.concatenate([stepped, jnp.zeros((1, 112), F32)], axis=1)
@@ -265,6 +285,7 @@
                 place(lay, why(ky), c),
             )))
     tile_dn[2 * row + core] = part_dn[core]
+    both(z2_take, 3, True)
     both(z2_take, 4, False)
     both(z2_take, 4, True)
     stepped, state = adapt(own_up[0, lay], v_mu[...], v_su[...])
@@ -417,15 +438,16 @@
         scratch_shapes=[
             vm(NY, NZ, 16, 1024), vm(NY, NZ, 16, 1024),
             vm(NZ, 2, 264, 128), vm(NZ, 2, 256, 128), vm(2, 1, 1024), vm(1, 1024),
-            vm(2, 3, 4, 16, 1024), vm(2, 7, 264, 128), vm(2, 7, 8, 1024),
-            vm(128, 640), vm(2, 3, 16, 640), vm(2, 16, 640),
+            vm(2, 3, 4, 16, 1024, t=BF16), vm(2, 7, 264, 128, t=BF16), vm(2, 7, 16, 512, t=BF16),
+            vm(2, 3, 4, 16, 1024, t=BF16), vm(2, 7, 264, 128, t=BF16), vm(2, 7, 16, 512, t=BF16),
+            vm(128, 640), vm(8, 16, 640, t=BF16), vm(2, NY, 16, 640, t=BF16), vm(2, 16, 640),
             vm(2, 16, 640, t=BF16), vm(8, 16, 640, t=BF16),
             vm(16, 1024), vm(16, 1024), vm(16, 1024), vm(16, 1024),
             vm(1, 16), vm(1, 16), vm(1, 16), vm(1, 16),
             dma((NY, 2)), dma((NZ, 2)), dma((10,)), dma((NY, 2)), dma((NZ, 2)), dma,
             dma((NY, 2)), dma((NZ, 2)), dma,
             dma((2, 3)), dma((2, 3)), dma((2, 7)), dma((2, 7)), dma((2, 7)), dma((2, 7)),
-            dma((2, 3)), dma((2, 3)), dma, dma,
+            dma((NY, 2)), dma((NY, 2)),
             dma((NY, 2)), dma((NY, 2)), dma((2, 7)), dma((2, 7)), dma((2, 7)), dma((2, 7)),
             dma((2, NZ)), dma((2, NZ)), dma((2, NZ)), dma((2, NZ)),
             dma((NZ,)), dma((NZ,)), dma((NY,)), dma((NY,)),

time: 74.2 us -> 64.5 us (0.87)
  Pallas kernels: 73.4 us -> 63.8 us
    pallas_call x1, Pallas kernels: 71.1 us -> 61.5 us  [on_device(): pl.pallas_call(kernel, out_shape=made, in_specs=[hbm] * 12, out_specs=(vm...]
where the time goes in v3:
time: 64.5 us; the launch traced here: 64.4 us
  Pallas kernels  63.8 us (99%)
  between operations  0.66 us (1%)
    pallas_call x1, Pallas kernels, on_device(): pl.pallas_call(kernel, out_shape=made, in_specs=[hbm] * 12, out_specs=(vm...  61.5 us
    pallas_call x1, Pallas kernels, on_device(): pl.pallas_call(writer, out_shape=(shape((NZ, NY, 2, 16, 1024), BF16), sha...  2.32 us

profile of v3, /device:TPU:1, one launch (start us, length us, event | category | flops | bytes accessed | tf_op | source)
XLA Modules:
  0.0 64.4 jit_solution(2521675986490212652)
XLA Ops:
  0.6 61.5 %reduce_step_gather.1 = (bf16[8,4,2,16,1024]{4,3,2,1,0:T(8,128)(2,1)S(1)}, bf16[8,2,528,128]{3,2,1,0:T(8,128)(2,1)S(1)}, f32[16,1024]{1,0:T(8,128)S(1)}, f32[16,...) custom-call(f32[8,4,2,16,1024]{4,3,2,1,0:T(8,128)} %bitcast.17, ...), custom_call_target="tpu_custom_call" | custom-call | tf_op jit(solution)/shard_map/reduce_step_gather/pallas_call | solution.py:433
  62.1 2.3 %write_out.1 = (bf16[8,4,2,16,1024]{4,3,2,1,0:T(8,128)(2,1)}, bf16[1024,1024]{1,0:T(8,128)(2,1)}, bf16[8,128]{1,0:T(8,128)(2,1)}, bf16[8,128]{1,0:T(8,128)(2,1)}...) custom-call(bf16[8,4,2,16,1024]{4,3,2,1,0:T(8,128)(2,1)S(1)} %get-tu, ...), custom_call_target="tpu_custom_call" | custom-call | tf_op jit(solution)/shard_map/write_out/pallas_call | solution.py:467

commit v4 on v3

v4 whole, which is shorter than its diff:
```python
import jax
import jax.numpy as jnp
from jax import lax
from jax.experimental import pallas as pl
from jax.experimental.pallas import tpu as pltpu
from jax.sharding import PartitionSpec as P

learn_rate = 0.05
hold_rate = 0.9
NZ, NY = 8, 4
MEAN_RATE = 64 ** (-0.5)
WAYS = ((0, 1), (1, -1))
F32, BF16 = jnp.float32, jnp.bfloat16


def adapt(total, master, memory):
    mean = total * MEAN_RATE
    state = hold_rate * memory + (1.0 - hold_rate) * mean * mean
    return master - learn_rate * mean * lax.rsqrt(state + 1e-06), state


def wrap(x, most):
    u = jnp.abs(x) * (224.0 / most)
    u2 = u * u
    u4 = u2 * u2
    u8 = u4 * u4
    y = jnp.where(u >= 1.0, u8 * u8, u8)
    return jnp.where(x < 0, -y, y).astype(BF16)


def unwrap(code, most):
    y = code.astype(F32)
    v = jnp.abs(y)
    q = lax.rsqrt(lax.rsqrt(jnp.maximum(v, 1e-37)))
    r8 = q * lax.rsqrt(q)
    r16 = r8 * lax.rsqrt(r8)
    r = jnp.where(v >= 1.0, r16, r8) * (most / 224.0)
    return jnp.where(y > 0, r, jnp.where(y < 0, -r, 0.0))


def slot_of(step, piece, half):
    if step == 1:
        return 0
    return 2 * step - (2 if piece == half else 3)


def kernel(
    up, dn, norm, bias, mu, md, mn, mb, su, sd, sn, sb,
    ou, od, o_tu, o_td, o_nu, o_nd, o_tn, o_tb, o_nn, o_nb,
    own_up, peer_up, own_dn, peer_dn, vecs, peer_vec,
    in_y, in_z, in_z2, to_y, to_z, to_z2, turned, to_yd, in_yd, pair,
    part_dn, tile_dn,
    v_mu, v_md, v_su, v_sd, v_mn, v_mb, v_sn, v_sb,
    join_in, vec_in, small_in, vec_out, join_out,
    y_in, z_in, z2_in, yd_in, tile_in, gz_in, uz_in, uy_in, uf_in, dgot, ugot,
    y_out, z_out, z2_out, yd_out, tile_out, gz_out, uz_out, uy_out, uf_out, dpass, upass,
):
    me = lax.axis_index("replica")
    core = lax.rem(me, 2)
    row = lax.rem(me // 2, NY)
    lay = me // (2 * NY)
    other = 1 - core

    def place(z, y, c):
        return {"replica": (z * NY + y) * 2 + c}

    def zed(k):
        return lax.rem(lay + k + 2 * NZ, NZ)

    def why(k):
        return lax.rem(row + k + 2 * NY, NY)

    peer = place(lay, row, other)
    z_next = [place(zed(way), row, core) for _, way in WAYS]
    y_next = [place(lay, why(way), core) for _, way in WAYS]

    def remote(src, dst, out, arrive, where):
        return pltpu.make_async_remote_copy(
            src_ref=src, dst_ref=dst, send_sem=out, recv_sem=arrive,
            device_id=where, device_id_type=pl.DeviceIdType.MESH,
        )

    def go(copy):
        copy.start()
        return copy

    def settle(ref, sem):
        pltpu.make_async_copy(ref, ref, sem).wait()

    smalls = [
        (norm, vecs.at[0]), (bias, vecs.at[1]), (mu, v_mu), (md, v_md), (su, v_su), (sd, v_sd),
        (mn, v_mn), (mb, v_mb), (sn, v_sn), (sb, v_sb),
    ]
    where = (0, 0, 1, 1, 1, 1, 2, 3, 4, 5)
    small_copies = [
        pltpu.make_async_copy(a, b, small_in.at[i]) for i, (a, b) in zip(where, smalls)
    ]
    for c in small_copies:
        c.start()

    def up_piece(ky, p, c):
        return up.at[pl.ds(4 * p, 4), why(ky), c]

    def dn_piece(k, p, c):
        rows = pl.multiple_of(c * 512 + p * 256, 256)
        return dn.at[pl.ds(rows, 256), pl.ds(pl.multiple_of(zed(k) * 128, 128), 128)]

    order = [
        ("d", 4, 0), ("d", 4, 1), ("u", 2, 0), ("u", 2, 1), ("d", 3, 1), ("d", 5, 0), ("d", 3, 0), ("d", 5, 1),
        ("u", 1, 1), ("u", 3, 0), ("u", 1, 0), ("u", 3, 1), ("d", 2, 1), ("d", 6, 0), ("d", 2, 0), ("d", 6, 1),
        ("d", 1, 1), ("d", 7, 0), ("d", 1, 0), ("d", 7, 1), ("u", 0, 0), ("u", 0, 1), ("d", 0, 0), ("d", 0, 1),
    ]
    loads, passes = [], []
    for i, (kind, k, p) in enumerate(order):
        sem = join_in.at[i // 2]
        if kind == "u":
            loads.append(pltpu.make_async_copy(
                up_piece(k, p, core), own_up.at[k, pl.ds(4 * p, 4)], sem
            ))
            passes.append(remote(
                up_piece(k, p, other), peer_up.at[k, pl.ds(4 * p, 4)], join_out.at[0], sem, peer
            ))
        else:
            loads.append(pltpu.make_async_copy(dn_piece(k, p, core), own_dn.at[k, p, pl.ds(0, 256)], sem))
            passes.append(remote(dn_piece(k, p, other), peer_dn.at[k, p], join_out.at[1], sem, peer))

    barrier = pltpu.get_barrier_semaphore()
    friends = [peer] + z_next
    for ky in (1, 2, 3):
        friends += [place(lay, why(ky), core), place(lay, why(ky), other)]
    for friend in friends:
        pl.semaphore_signal(barrier, inc=1, device_id=friend, device_id_type=pl.DeviceIdType.MESH)
    for copy in loads:
        copy.start()
    pl.semaphore_wait(barrier, len(friends))
    settle(vecs, small_in.at[0])
    vec_pass = go(remote(vecs.at[other], peer_vec, vec_out, vec_in, peer))
    for copy in passes:
        go(copy)

    vec_pass.wait_recv()
    peer_vec[...] = 0.5 * (vecs[core] + peer_vec[...])

    def join(i):
        pair_of = order[2 * i : 2 * i + 2]
        settle((peer_up if pair_of[0][0] == "u" else peer_dn).at[pl.ds(0, 2)], join_in.at[i])
        for kind, k, p in pair_of:
            if kind == "u":
                own_up[k, 4 * p : 4 * p + 4] += peer_up[k, 4 * p : 4 * p + 4]
            else:
                own_dn[k, p, 0:256] += peer_dn[k, p]
                line = peer_vec[:, pl.ds(pl.multiple_of(zed(k) * 128, 128), 128)]
                own_dn[k, p, 256:264] = jnp.broadcast_to(line, (8, 128))

    def reducer(count, mine, leave, arrive, out, inn, neighbour, most):
        reach = count // 2

        def chunk(way, step):
            return (way * (reach + 1 - step)) % count

        def copy_of(way, step, piece):
            di = way[0]
            slot = slot_of(step, piece, di)
            return remote(leave.at[di, slot], arrive.at[di, slot], out, inn.at[di, slot], neighbour[di])

        def post(way, step, piece, value):
            di = way[0]
            leave[di, slot_of(step, piece, di)] = wrap(value, most * (step if piece == di else step - 1))
            go(copy_of(way, step, piece))

        def send(way, step, piece):
            post(way, step, piece, mine(chunk(way[1], step), piece)[...])

        def take(way, step, piece):
            di, direction = way
            copy_of(way, step, piece).wait_recv()
            ref = mine(chunk(direction, step + 1), piece)
            sofar = most * (step if piece == di else step - 1)
            total = ref[...] + unwrap(arrive[di, slot_of(step, piece, di)], sofar)
            if step < reach:
                post(way, step + 1, piece, total)
            else:
                ref[...] = total

        return send, take

    z_send, z_take = reducer(
        NZ, lambda k, p: own_dn.at[k, p], to_z, in_z, z_out, z_in, z_next, 16.0
    )
    y_send, y_take = reducer(
        NY, lambda k, p: own_up.at[k, pl.ds(4 * p, 4)], to_y, in_y, y_out, y_in, y_next, 16.0
    )
    z2_send, z2_take = reducer(
        NZ, lambda k, p: own_up.at[0, zed(k), :, pl.ds(512 * p, 512)],
        to_z2, in_z2, z2_out, z2_in, z_next, 64.0,
    )

    def both(act, step, near):
        for way in WAYS:
            act(way, step, way[0] if near else 1 - way[0])

    join(0)
    both(z_send, 1, True)
    join(1)
    both(y_send, 1, True)
    join(2)
    both(z_send, 2, False)
    join(3)
    join(4)
    both(z_take, 1, True)
    both(y_send, 2, False)
    join(5)
    join(6)
    both(z_take, 2, False)
    join(7)
    both(y_take, 1, True)
    both(z_take, 2, True)
    join(8)
    both(z_take, 3, False)
    join(9)
    join(10)
    both(y_take, 2, False)
    both(z_take, 3, True)
    join(11)
    both(y_take, 2, True)
    both(z2_send, 1, True)
    both(z_take, 4, False)
    both(z2_send, 2, False)
    both(z_take, 4, True)

    for p in (0, 1):
        turned[:, 256 * p : 256 * p + 256] = own_dn[0, p, 0:256].T
    turned[:, 512:640] = own_dn[0, 0, 136:264].T
    to_yd[...] = wrap(turned[...], 128.0).reshape(8, 16, 640)
    others = [(ky, x) for ky in (2, 1, 3, 0) for x in (0, 1) if (ky, x) != (0, 0)]
    for ky, x in others:
        c = core if x == 0 else other
        go(remote(
            to_yd.at[2 * why(ky) + c], in_yd.at[NY * core + ky], yd_out, yd_in, place(lay, why(ky), c)
        ))
    settle(own_up.at[1, pl.ds(0, 4)], small_in.at[1])
    for i in range(2, 6):
        small_copies[4 + i].wait()
    both(z2_take, 1, True)
    both(z2_take, 2, False)
    both(z2_take, 2, True)
    settle(in_yd.at[pl.ds(1, 7)], yd_in)

    def came(c, ky):
        return unwrap(in_yd[NY * c + ky], 128.0)

    pair[core] = turned[pl.ds(pl.multiple_of(16 * (2 * row + core), 16), 16), :] + (
        came(core, 1) + came(core, 2) + came(core, 3)
    )
    pair[other] = came(other, 0) + came(other, 1) + came(other, 2) + came(other, 3)
    lines = ((v_mn, v_sn, o_tn, o_nn), (v_mb, v_sb, o_tb, o_nb))
    for r in (0, 1):
        cols = slice(512 * r, 512 * r + 512)
        stepped, state = adapt(pair[r, :, 0:512], v_md[:, cols], v_sd[:, cols])
        o_td[:, cols] = stepped
        o_nd[:, cols] = state
        part_dn[r, :, 0:512] = stepped.astype(BF16)
        block = jnp.concatenate([pair[r, :, 512:640], jnp.zeros((112, 128), F32)], axis=0).T
        master, memory, o_t, o_n = lines[r]
        stepped, state = adapt(2.0 * block[127:128, 0:16], master[...], memory[...])
        o_t[...] = stepped
        o_n[...] = state
        wide = jnp.concatenate([stepped, jnp.zeros((1, 112), F32)], axis=1)
        part_dn[r, :, 512:640] = jnp.broadcast_to(wide, (128, 128)).T[0:16].astype(BF16)

    for ky, x in others:
        c = core if x == 0 else other
        go(remote(
            part_dn.at[c], tile_dn.at[2 * row + core], tile_out, tile_in, place(lay, why(ky), c)
        ))
    tile_dn[2 * row + core] = part_dn[core]

    both(z2_take, 3, False)
    both(z2_take, 3, True)
    both(z2_take, 4, False)
    both(z2_take, 4, True)
    stepped, state = adapt(own_up[0, lay], v_mu[...], v_su[...])
    o_tu[...] = stepped
    o_nu[...] = state
    ou[lay, row, core] = stepped.astype(BF16)

    def spread_up(way, step, piece):
        di, direction = way
        ref = ou.at[zed(-direction * (step - 1)), row, core, :, pl.ds(512 * piece, 512)]
        slot = 2 * step - (2 if piece == di else 1)
        return remote(ref, ref, uz_out, uz_in.at[di, slot], z_next[di])

    def aside(di, kz):
        ref = ou.at[zed(kz), row, core]
        return remote(ref, ref, uy_out, uy_in.at[kz % NZ], y_next[di])

    def aside_far(way, kz):
        di, direction = way
        ref = ou.at[zed(kz), why(-direction), core, :, pl.ds(512 * di, 512)]
        return remote(ref, ref, uf_out, uf_in.at[kz % NZ], y_next[di])

    def across_up(kz, ky):
        ref = ou.at[zed(kz), why(ky), core]
        return remote(ref, ref, upass, ugot, peer)

    def share(kz):
        for di in (0, 1):
            go(aside(di, kz))
        go(across_up(kz, 0))

    def turn(kz):
        settle(ou.at[0, pl.ds(0, 2), 0], uy_in.at[kz % NZ])
        for way in WAYS:
            go(aside_far(way, kz))
        for way in WAYS:
            go(across_up(kz, -way[1]))

    def turned_far(kz):
        settle(ou.at[0, 0, 0], uf_in.at[kz % NZ])
        go(across_up(kz, 2))

    def spread_dn(way, step, piece):
        di, direction = way
        rows = pl.ds(0, 256) if piece == 0 else pl.ds(256, 272)
        ref = od.at[zed(-direction * (step - 1)), core, rows]
        slot = 2 * step - (2 if piece == di else 1)
        return remote(ref, ref, gz_out, gz_in.at[di, slot], z_next[di])

    def across_dn(k):
        ref = od.at[zed(k), core]
        return remote(ref, ref, dpass, dgot, peer)

    def onward(spread, step, near):
        for way in WAYS:
            piece = way[0] if near else 1 - way[0]
            spread(way, step, piece).wait_recv()
            if step < 3 or (step == 3 and near):
                go(spread(way, step + 1, piece))

    def up_step(step):
        onward(spread_up, step, True)
        if step < 4:
            onward(spread_up, step, False)
            share(step)
        share(-step) if step < 4 else share(4)

    for near in (True, False):
        for way in WAYS:
            go(spread_up(way, 1, way[0] if near else 1 - way[0]))
    share(0)
    settle(tile_dn.at[pl.ds(0, 7)], tile_in)
    for j in range(5):
        flat = tile_dn[:, :, 128 * j : 128 * j + 128].astype(F32).reshape(128, 128).T.astype(BF16)
        if j < 4:
            od[lay, core, 128 * j : 128 * j + 128] = flat
        else:
            od[lay, core, 512:528] = flat[112:128]
    for way in WAYS:
        go(spread_dn(way, 1, way[0]))
    go(across_dn(0))
    up_step(1)
    for way in WAYS:
        go(spread_dn(way, 1, 1 - way[0]))
    up_step(2)
    onward(spread_dn, 1, True)
    turn(0)
    onward(spread_dn, 1, False)
    go(across_dn(1))
    go(across_dn(-1))
    up_step(3)
    turn(1)
    turn(-1)
    onward(spread_dn, 2, True)
    turned_far(0)
    up_step(4)
    onward(spread_dn, 2, False)
    go(across_dn(2))
    go(across_dn(-2))
    turn(2)
    turn(-2)
    turned_far(1)
    turned_far(-1)
    onward(spread_dn, 3, True)
    turn(3)
    turn(-3)
    turned_far(2)
    turned_far(-2)
    turn(4)
    onward(spread_dn, 3, False)
    go(across_dn(3))
    go(across_dn(-3))
    turned_far(3)
    turned_far(-3)
    turned_far(4)
    onward(spread_dn, 4, True)
    go(across_dn(4))

    settle(peer_vec, vec_out)
    settle(peer_up, join_out.at[0])
    settle(peer_dn, join_out.at[1])
    settle(to_y, y_out)
    settle(to_z, z_out)
    settle(to_z2, z2_out)
    settle(to_yd.at[pl.ds(0, 7)], yd_out)
    settle(tile_dn.at[pl.ds(0, 7)], tile_out)
    settle(od.at[pl.ds(0, 7), 0], gz_out)
    settle(to_z2, uz_out)
    settle(ou.at[:, pl.ds(0, 2), 0], uy_out)
    settle(ou.at[:, 0, 0], uf_out)
    settle(ou.at[:, :, 0], upass)
    settle(od.at[:, 0], dpass)
    settle(ou.at[:, :, other], ugot)
    settle(od.at[:, other], dgot)


def writer(
    ou, od, o_tu, o_td, o_nu, o_nd, o_tn, o_tb, o_nn, o_nb,
    cu, cd, cn, cb, tu, td, tn, tb, nu, nd, nn, nb,
    v_cn, v_cb, sem,
):
    pairs = [(ou, cu)]
    for z in range(NZ):
        for r in (0, 1):
            pairs.append((
                od.at[z, r, pl.ds(0, 512)], cd.at[pl.ds(512 * r, 512), pl.ds(128 * z, 128)]
            ))
    pairs += [
        (o_tu, tu), (o_td, td), (o_nu, nu), (o_nd, nd), (o_tn, tn), (o_tb, tb), (o_nn, nn), (o_nb, nb),
        (v_cn, cn), (v_cb, cb),
    ]
    copies = [pltpu.make_async_copy(a, b, sem.at[i]) for i, (a, b) in enumerate(pairs)]
    for copy in copies[:-2]:
        copy.start()
    for r, line in enumerate((v_cn, v_cb)):
        rows = [od[z, r, 520:528].astype(F32)[7:8] for z in range(NZ)]
        line[...] = jnp.concatenate(rows, axis=0).astype(BF16)
    for copy in copies[-2:]:
        copy.start()
    for copy in copies:
        copy.wait()


def on_device(
    partial_up, partial_down, partial_norm, partial_bias,
    master_up, master_down, master_norm, master_bias,
    memory_up, memory_down, memory_norm, memory_bias,
):
    def shape(s, t=F32):
        return jax.ShapeDtypeStruct(s, t)

    def vm(*s, t=F32):
        return pltpu.VMEM(s, t)

    dma = pltpu.SemaphoreType.DMA
    hbm = pl.BlockSpec(memory_space=pltpu.HBM)
    vmem = pl.BlockSpec(memory_space=pltpu.VMEM)
    made = (
        pltpu.VMEM((NZ, NY, 2, 16, 1024), BF16), pltpu.VMEM((NZ, 2, 528, 128), BF16),
        vm(16, 1024), vm(16, 1024), vm(16, 1024), vm(16, 1024),
        vm(1, 16), vm(1, 16), vm(1, 16), vm(1, 16),
    )
    made = pl.pallas_call(
        kernel,
        out_shape=made,
        in_specs=[hbm] * 12,
        out_specs=(vmem,) * 10,
        scratch_shapes=[
            vm(NY, NZ, 16, 1024), vm(NY, NZ, 16, 1024),
            vm(NZ, 2, 264, 128), vm(NZ, 2, 256, 128), vm(2, 1, 1024), vm(1, 1024),
            vm(2, 3, 4, 16, 1024, t=BF16), vm(2, 7, 264, 128, t=BF16), vm(2, 7, 16, 512, t=BF16),
            vm(2, 3, 4, 16, 1024, t=BF16), vm(2, 7, 264, 128, t=BF16), vm(2, 7, 16, 512, t=BF16),
            vm(128, 640), vm(8, 16, 640, t=BF16), vm(2 * NY, 16, 640, t=BF16), vm(2, 16, 640),
            vm(2, 16, 640, t=BF16), vm(8, 16, 640, t=BF16),
            vm(16, 1024), vm(16, 1024), vm(16, 1024), vm(16, 1024),
            vm(1, 16), vm(1, 16), vm(1, 16), vm(1, 16),
            dma((12,)), dma, dma((6,)), dma, dma((2,)),
            dma((2, 3)), dma((2, 7)), dma((2, 7)), dma, dma, dma((2, 7)), dma((2, 7)), dma((NZ,)), dma((NZ,)), dma, dma,
            dma, dma, dma, dma, dma, dma, dma, dma, dma, dma, dma,
        ],
        compiler_params=pltpu.CompilerParams(
            collective_id=0, has_side_effects=True, vmem_limit_bytes=32 * 1024 * 1024
        ),
        name="reduce_step_gather",
    )(*(
        pltpu.with_memory_space_constraint(a, pltpu.HBM)
        for a in (
            partial_up.reshape(NZ, NY, 2, 16, 1024), partial_down[0], partial_norm, partial_bias,
            master_up, master_down.T, master_norm[None], master_bias[None],
            memory_up, memory_down.T, memory_norm[None], memory_bias[None],
        )
    ))
    out = pl.pallas_call(
        writer,
        out_shape=(
            shape((NZ, NY, 2, 16, 1024), BF16), shape((1024, 1024), BF16),
            shape((8, 128), BF16), shape((8, 128), BF16),
            shape((16, 1024)), shape((16, 1024)), shape((1, 16)), shape((1, 16)),
            shape((16, 1024)), shape((16, 1024)), shape((1, 16)), shape((1, 16)),
        ),
        in_specs=[vmem] * 10,
        out_specs=(hbm,) * 12,
        scratch_shapes=[vm(8, 128, t=BF16), vm(8, 128, t=BF16), dma((27,))],
        compiler_params=pltpu.CompilerParams(vmem_limit_bytes=32 * 1024 * 1024),
        name="write_out",
    )(*made)
    cu, cd, cn, cb, tu, td, tn, tb, nu, nd, nn, nb = out
    return (
        cu.reshape(1024, 1024), cd, cn.reshape(1024), cb.reshape(1024),
        tu, td.T, tn[0], tb[0], nu, nd.T, nn[0], nb[0],
    )


def solution(mesh):
    in_specs = (
        P("replica", None, "model"), P("replica", "model", None), P("replica", None), P("replica", None),
        P("replica", "model"), P("model", "replica"), P("replica"), P("replica"),
        P("replica", "model"), P("model", "replica"), P("replica"), P("replica"),
    )
    out_specs = (
        P(None, "model"), P("model", None), P(), P(),
        P("replica", "model"), P("model", "replica"), P("replica"), P("replica"),
        P("replica", "model"), P("model", "replica"), P("replica"), P("replica"),
    )
    return jax.shard_map(
        on_device, mesh=mesh, in_specs=in_specs, out_specs=out_specs, check_vma=False
    )
```

time: 64.5 us -> 61.8 us (0.958)
  Pallas kernels: 63.8 us -> 61.1 us
    pallas_call x1, Pallas kernels: 61.5 us -> 58.7 us  [on_device(): pl.pallas_call(kernel, out_shape=made, in_specs=[hbm] * 12, out_specs=(vm...]
where the time goes in v4:
time: 61.8 us; the launch traced here: 61.7 us
  Pallas kernels  61.1 us (99%)
  between operations  0.66 us (1%)
    pallas_call x1, Pallas kernels, on_device(): pl.pallas_call(kernel, out_shape=made, in_specs=[hbm] * 12, out_specs=(vm...  58.7 us
    pallas_call x1, Pallas kernels, on_device(): pl.pallas_call(writer, out_shape=(shape((NZ, NY, 2, 16, 1024), BF16), sha...  2.32 us

profile of v4, /device:TPU:1, one launch (start us, length us, event | category | flops | bytes accessed | tf_op | source)
XLA Modules:
  0.0 61.7 jit_solution(9861047469544548918)
XLA Ops:
  0.6 58.7 %reduce_step_gather.1 = (bf16[8,4,2,16,1024]{4,3,2,1,0:T(8,128)(2,1)S(1)}, bf16[8,2,528,128]{3,2,1,0:T(8,128)(2,1)S(1)}, f32[16,1024]{1,0:T(8,128)S(1)}, f32[16,...) custom-call(f32[8,4,2,16,1024]{4,3,2,1,0:T(8,128)} %bitcast.17, ...), custom_call_target="tpu_custom_call" | custom-call | tf_op jit(solution)/shard_map/reduce_step_gather/pallas_call | solution.py:462
  59.4 2.3 %write_out.1 = (bf16[8,4,2,16,1024]{4,3,2,1,0:T(8,128)(2,1)}, bf16[1024,1024]{1,0:T(8,128)(2,1)}, bf16[8,128]{1,0:T(8,128)(2,1)}, bf16[8,128]{1,0:T(8,128)(2,1)}...) custom-call(bf16[8,4,2,16,1024]{4,3,2,1,0:T(8,128)(2,1)S(1)} %get-tu, ...), custom_call_target="tpu_custom_call" | custom-call | tf_op jit(solution)/shard_map/write_out/pallas_call | solution.py:492
